TPU v7x, 512 devices: a whole 4x8x8 slice. The times are simulated.
512 devices in a mesh: gx: 16 (over y_lo, z), gy: 4 (over x), col: 8 (over y_hi, core).
Axes of the slice: x: 4, y: 8 (y_hi: 4, y_lo: 2; y = y_hi * 2 + y_lo), z: 8, core: 2. Of those that a mesh axis runs over, the one named last changes fastest.
Arguments:
- fields: bfloat16 [8, 128, 128, 32, 128], P('col', 'gx', 'gy'), may hold values from -6 to 6
- spectral: bfloat16 [1, 16, 16, 2, 32, 32, 16], P(None, 'gx', 'gy', None, None, 'col'), may hold values from -0.75 to 0.75
- skip_weight: bfloat16 [1, 32, 32], replicated, may hold values from -1 to 1
- skip_bias: float32 [1, 32], replicated, may hold values from -3 to 3
- norm_gain: float32 [1, 32], replicated, may hold values from 0.5 to 1.5
- norm_shift: float32 [1, 32], replicated, may hold values from -3 to 3
Outputs:
- activations: bfloat16 [8, 128, 128, 32, 128], P('col', 'gx', 'gy')
All inputs are finite; a program needn't handle non-finite values.
Results may differ from a plain program's by a relative error of at most 0.012.
Values may be sent and summed in bfloat16 or wider, within the bound.
A program may use at most 64 MiB of HBM per device.

v0:
```python
import math

import jax
import jax.numpy as jnp
from jax import lax
from jax.sharding import PartitionSpec as P

X = 128
Y = 128
Z = 128
MX = 16
MY = 16
MZ = 16


norm_eps = 1e-05


def cut_along(shard, dim, length):
    before, after = (shard.shape[:dim], shard.shape[dim + 1 :])
    return jnp.moveaxis(shard.reshape(*before, length, -1, *after), dim, 0)


def summed_on_arrival(shard, axis, dim):
    length = lax.axis_size(axis)
    parts = lax.all_to_all(cut_along(shard, dim, length), axis, 0, 0, tiled=True)
    return jnp.sum(parts.astype(jnp.float32), axis=0)


def copy_for_each(shard, axis):
    copies = jnp.broadcast_to(shard, (lax.axis_size(axis), *shard.shape))
    return lax.all_to_all(copies, axis, split_axis=0, concat_axis=0, tiled=True)


def joined_along(parts, dim):
    shape = list(parts.shape[1:])
    shape[dim] *= parts.shape[0]
    return jnp.moveaxis(parts, 0, dim).reshape(shape)


def collect(shard, axis, dim):
    parts = copy_for_each(shard, axis)
    return joined_along(parts, dim)


def signed_freqs(count):
    index = jnp.arange(count, dtype=jnp.int32)
    return jnp.where(index < count // 2, index, index - count)


def angles(positions, frequency, length):
    turn_count = positions[:, None] * frequency[None, :] % length
    return turn_count.astype(jnp.float32) * (2.0 * math.pi / length)


def forward_table(positions, frequency, length, factor):
    phase_angle = angles(positions, frequency, length)
    cosine = jnp.cos(phase_angle) * factor
    sine_part = jnp.sin(phase_angle) * factor
    from_real = jnp.stack([cosine, -sine_part], axis=-1)
    from_imag = jnp.stack([sine_part, cosine], axis=-1)
    return jnp.stack([from_real, from_imag], axis=1)


def inverse_table(frequency, positions, length):
    phase_angle = angles(positions, frequency, length).T
    cosine = jnp.cos(phase_angle)
    sine_part = jnp.sin(phase_angle)
    from_real = jnp.stack([cosine, sine_part], axis=-1)
    from_imag = jnp.stack([-sine_part, cosine], axis=-1)
    return jnp.stack([from_real, from_imag], axis=1)


def depth_tables(length, count):
    frequency = jnp.arange(count, dtype=jnp.int32)
    phase_angle = angles(jnp.arange(length, dtype=jnp.int32), frequency, length)
    forward = jnp.concatenate([jnp.cos(phase_angle), -jnp.sin(phase_angle)], axis=1)
    backward = jnp.concatenate([jnp.cos(phase_angle).T, -jnp.sin(phase_angle).T], axis=0)
    return (forward.astype(jnp.bfloat16), backward.astype(jnp.bfloat16))


def mix_modes(spectrum, weight):

    def contract(left, right):
        return jnp.einsum("abcz,abcdz->abdz", left, right, preferred_element_type=jnp.float32)

    real_in = spectrum[:, :, :, 0]
    imag_in = spectrum[:, :, :, 1]
    real_weight = weight[:, :, 0]
    imag_weight = weight[:, :, 1]
    real_out = contract(real_in, real_weight) - contract(imag_in, imag_weight)
    imag_out = contract(real_in, imag_weight) + contract(imag_in, real_weight)
    return jnp.stack([real_out, imag_out], axis=3)


def finish(spectral_part, skip_part, offset, scaling, shift_term):
    pre_norm = spectral_part + skip_part + offset[:, None]
    centre = jnp.mean(pre_norm, axis=2, keepdims=True)
    spread = jnp.mean(jnp.square(pre_norm - centre), axis=2, keepdims=True)
    normed = (pre_norm - centre) * lax.rsqrt(spread + norm_eps) * scaling[:, None] + shift_term[
        :, None
    ]
    return jax.nn.gelu(normed, approximate=False).astype(jnp.bfloat16)


def local(fields, spectral, skip_weight, skip_bias, norm_gain, norm_shift):
    hidden = fields[0]
    tile_first, tile_second, channels, depth_cells = hidden.shape
    first_cells = lax.axis_index("gx") * tile_first + jnp.arange(tile_first, dtype=jnp.int32)
    second_cells = lax.axis_index("gy") * tile_second + jnp.arange(tile_second, dtype=jnp.int32)
    depth_forward, depth_backward = depth_tables(Z, MZ)
    second_forward = forward_table(second_cells, signed_freqs(MY), Y, 1.0).astype(jnp.bfloat16)
    first_forward = forward_table(first_cells, signed_freqs(MX), X, 1.0 / math.sqrt(X * Y * Z))
    first_inverse = inverse_table(signed_freqs(MX), first_cells, X).astype(jnp.bfloat16)
    second_inverse = inverse_table(signed_freqs(MY), second_cells, Y)
    inverse_scale = 1.0 / math.sqrt(MX * MY * MZ)
    amplitude = jnp.dot(
        hidden.reshape(-1, depth_cells), depth_forward, preferred_element_type=jnp.float32
    )
    amplitude = amplitude.astype(jnp.bfloat16).reshape(tile_first, tile_second, channels, 2, MZ)
    along_second = jnp.einsum(
        "xycrz,yrks->xkcsz", amplitude, second_forward, preferred_element_type=jnp.float32
    )
    summed_second = summed_on_arrival(along_second.astype(jnp.bfloat16), "gy", 1)
    partial_modes = jnp.einsum("xkcsz,xsjt->jkctz", summed_second, first_forward)
    summed = summed_on_arrival(partial_modes.astype(jnp.bfloat16), "gx", 0)
    spectrum = summed.astype(jnp.bfloat16)
    weights_here = spectral[0]
    mixed_modes = mix_modes(spectrum, collect(weights_here, "col", 4)).astype(jnp.bfloat16)
    gathered_second = collect(mixed_modes, "gy", 1)
    full_modes = collect(gathered_second, "gx", 0)
    rows_first = jnp.einsum(
        "jkcsz,jsxt->xkctz", full_modes, first_inverse, preferred_element_type=jnp.float32
    )
    rows_both = jnp.einsum("xkcsz,ksyt->xyctz", rows_first, second_inverse).astype(jnp.bfloat16)
    spectral_part = jnp.dot(
        rows_both.reshape(-1, 2 * MZ), depth_backward, preferred_element_type=jnp.float32
    )
    spectral_part = (
        spectral_part.reshape(tile_first, tile_second, channels, depth_cells) * inverse_scale
    )
    skip_part = jnp.einsum(
        "oc,xycz->xyoz", skip_weight[0], hidden, preferred_element_type=jnp.float32
    )
    hidden = finish(spectral_part, skip_part, skip_bias[0], norm_gain[0], norm_shift[0])
    return hidden[None]


def solution(mesh):
    placed = (
        P("col", "gx", "gy", None, None),
        P(None, "gx", "gy", None, None, "col", None),
        P(),
        P(),
        P(),
        P(),
    )
    return jax.shard_map(
        local,
        mesh=mesh,
        in_specs=placed,
        out_specs=P("col", "gx", "gy", None, None),
        check_vma=False,
    )
```

profile of v0, /device:TPU:24, one launch (start us, length us, event | category | flops | bytes accessed | tf_op | source)
XLA Modules:
  0.0 119.3 jit_solution(9642873758831152271)
XLA Ops:
  0.1 1.5 %copy-done = bf16[1,8,32,32,128]{4,3,2,1,0:T(8,128)(2,1)S(1)} copy-done((bf16[1,8,32,32,128]{4,3,2,1,0:T(8,128)(2,1)S(1)}, bf16[1,8,32,32,128]{4,3,2,1,0:T(8,128)(2,1)}, u32[]{:S(2)}) %copy-start) | copy-done | bytes 2097176
  1.6 0.8 fusion
  2.4 2.6 %reshape.787 = bf16[8,32,32,2,16]{2,1,0,4,3:T(8,128)(2,1)} reshape(bf16[8192,32]{0,1:T(8,128)(2,1)S(1)} %fusion) | data formatting | bytes 1048576 | tf_op jit(solution)/shard_map/reshape | solution.py:120
  5.0 0.1 negate_convert_fusion.2
  5.2 2.1 %bitcast_convert_fusion.1 = bf16[16,2,8,32,16]{3,0,4,2,1:T(8,128)(2,1)S(1)} fusion(bf16[8,32,32,2,16]{2,1,0,4,3:T(8,128)(2,1)} %reshape.787, bf16[32,1,16,2]{0,2,1,3:T(8,128)(2,1)S(1)} %get-tuple-element.12, bf16[32,1,16,2]{0,2,1,3:T(8,128)(2,1)S(1)} %get-tuple-element.11), kind=kOutput, calls=%fused_computation.30 | convolution fusion | flops 16916480 | bytes 790528 | tf_op jit(solution)/shard_map/xycrz,yrks->xkcsz/dot_general | solution.py:121
  7.2 0.6 copy.110
  7.8 1.7 %reshape.818 = bf16[4,2,16384]{2,1,0:T(2,128)(2,1)} reshape(bf16[4,2,8,16,4,32]{5,4,3,2,1,0:T(4,128)(2,1)S(1)} %bitcast.195) | data formatting | bytes 524288
  9.5 4.3 %all-to-all-start = ((bf16[4,2,16384]{2,1,0:T(2,128)(2,1)}), bf16[4,2,16384]{2,1,0:T(2,128)(2,1)S(1)}, u32[]{:S(2)}, u32[]{:S(2)}) async-start(bf16[4,2,16384]{2,1,0:T(2,128)(2,1)} %reshape.818), calls=%async_computation | async-start | bytes 524288 | tf_op jit(solution)/shard_map/all_to_all | solution.py:26
  13.8 0.1 fusion.87
  13.9 6.5 %all-to-all-done = bf16[4,2,16384]{2,1,0:T(2,128)(2,1)S(1)} async-done(((bf16[4,2,16384]{2,1,0:T(2,128)(2,1)}), bf16[4,2,16384]{2,1,0:T(2,128)(2,1)S(1)}, u32[]{:S(2)}, u32[]{:S(2)}) %all-to-all-start) | async-done | bytes 262176 | tf_op jit(solution)/shard_map/all_to_all | solution.py:26
  20.5 0.5 reshape.819
  21.0 0.2 convert_reduce_fusion
  21.2 0.4 fusion.31
  21.5 0.1 copy.111
  21.7 1.2 reshape.820
  22.9 11.8 %all-to-all-start.1 = ((bf16[16,2,2048]{2,1,0:T(2,128)(2,1)}), bf16[16,2,2048]{2,1,0:T(2,128)(2,1)S(1)}, u32[]{:S(2)}, u32[]{:S(2)}) async-start(bf16[16,2,2048]{2,1,0:T(2,128)(2,1)} %reshape.820), calls=%async_computation.1 | async-start | bytes 262144 | tf_op jit(solution)/shard_map/all_to_all | solution.py:26
  34.7 1.1 broadcast_bitcast_fusion.1
  35.8 1.7 %reshape.816 = bf16[8,2,8192]{2,1,0:T(2,128)(2,1)} reshape(bf16[8,1,4,2,4,16,32]{6,5,4,3,2,1,0:T(8,128)(2,1)S(1)} %broadcast_bitcast_fusion.1) | data formatting | bytes 524288
  37.5 4.8 %all-to-all-done.1 = bf16[16,2,2048]{2,1,0:T(2,128)(2,1)S(1)} async-done(((bf16[16,2,2048]{2,1,0:T(2,128)(2,1)}), bf16[16,2,2048]{2,1,0:T(2,128)(2,1)S(1)}, u32[]{:S(2)}, u32[]{:S(2)}) %all-to-all-start.1) | async-done | bytes 131104 | tf_op jit(solution)/shard_map/all_to_all | solution.py:26
  42.2 6.5 %all-to-all-start.2 = ((bf16[8,2,8192]{2,1,0:T(2,128)(2,1)}), bf16[8,2,8192]{2,1,0:T(2,128)(2,1)S(1)}, u32[]{:S(2)}, u32[]{:S(2)}) async-start(bf16[8,2,8192]{2,1,0:T(2,128)(2,1)} %reshape.816), calls=%async_computation.2 | async-start | bytes 524288 | tf_op jit(solution)/shard_map/all_to_all | solution.py:32
  48.8 0.3 reshape.821
  49.2 9.5 %all-to-all-done.2 = bf16[8,2,8192]{2,1,0:T(2,128)(2,1)S(1)} async-done(((bf16[8,2,8192]{2,1,0:T(2,128)(2,1)}), bf16[8,2,8192]{2,1,0:T(2,128)(2,1)S(1)}, u32[]{:S(2)}, u32[]{:S(2)}) %all-to-all-start.2) | async-done | bytes 262176 | tf_op jit(solution)/shard_map/all_to_all | solution.py:32
  58.6 0.5 reshape.817
  59.2 0.2 copy.45
  59.4 0.2 slice_bitcast_fusion.1
  59.6 1.2 %copy.56 = bf16[4,32,32,16]{2,1,3,0:T(8,128)(2,1)} copy(bf16[4,32,32,16]{1,3,2,0:T(8,128)(2,1)S(1)} %get-tuple-element.5) | data formatting | bytes 262144 | tf_op jit(solution)/shard_map/reshape.1
  60.8 0.5 copy.59
  61.3 1.3 %fusion.34 = f32[4,16,1,32]{3,2,1,0:T(1,128)S(1)} fusion(bf16[4,32,32,16]{2,1,3,0:T(8,128)(2,1)} %copy.56, bf16[4,32,16,1]{1,2,0,3:T(8,128)(2,1)S(1)} %get-tuple-element.7), kind=kOutput, calls=%fused_computation.55 | convolution fusion | flops 131072 | bytes 143360 | tf_op jit(solution)/shard_map/abcz,abcdz->abdz/dot_general | solution.py:85
  62.6 1.3 %fusion.40 = f32[4,16,1,32]{3,2,1,0:T(1,128)S(1)} fusion(bf16[4,32,32,16]{2,1,3,0:T(8,128)(2,1)} %copy.56, bf16[4,32,16,1]{1,2,0,3:T(8,128)(2,1)S(1)} %get-tuple-element.8), kind=kOutput, calls=%fused_computation.61 | convolution fusion | flops 131072 | bytes 143360 | tf_op jit(solution)/shard_map/abcz,abcdz->abdz/dot_general | solution.py:85
  63.9 0.3 fusion.38
  64.1 0.3 fusion.36
  64.5 0.2 reshape.822
  64.6 7.8 %all_to_all.25 = bf16[4,2,2048]{2,1,0:T(2,128)(2,1)S(1)} all-to-all(bf16[4,2,2048]{2,1,0:T(2,128)(2,1)S(1)} %reshape.822), channel_id=1, replica_groups=mesh['gx'=16,'gy'=4,'col'=8] {'gy'}, dimensions={0} | all-to-all | bytes 65536 | tf_op jit(solution)/shard_map/all_to_all | solution.py:32
  72.4 0.1 reshape.823
  72.6 1.7 %broadcast_bitcast_fusion = bf16[16,1,16,2,16,32]{5,4,3,2,1,0:T(8,128)(2,1)} fusion(bf16[16,32,2,16]{1,3,2,0:T(8,128)(2,1)S(1)} %bitcast.199), kind=kLoop, calls=%fused_computation.169 | loop fusion | bytes 557056
  74.3 4.5 %reshape.824 = bf16[16,2,8192]{2,1,0:T(2,128)(2,1)} reshape(bf16[16,1,16,2,16,32]{5,4,3,2,1,0:T(8,128)(2,1)} %broadcast_bitcast_fusion) | data formatting | bytes 1048576
  78.8 5.0 %all-to-all-start.4 = ((bf16[16,2,8192]{2,1,0:T(2,128)(2,1)}), bf16[16,2,8192]{2,1,0:T(2,128)(2,1)S(1)}, u32[]{:S(2)}, u32[]{:S(2)}) async-start(bf16[16,2,8192]{2,1,0:T(2,128)(2,1)} %reshape.824), calls=%async_computation.4 | async-start | bytes 1048576 | tf_op jit(solution)/shard_map/all_to_all | solution.py:32
  83.9 0.1 fusion.86
  84.0 0.1 fusion.82
  84.1 13.9 %all-to-all-done.4 = bf16[16,2,8192]{2,1,0:T(2,128)(2,1)S(1)} async-done(((bf16[16,2,8192]{2,1,0:T(2,128)(2,1)}), bf16[16,2,8192]{2,1,0:T(2,128)(2,1)S(1)}, u32[]{:S(2)}, u32[]{:S(2)}) %all-to-all-start.4) | async-done | bytes 524320 | tf_op jit(solution)/shard_map/all_to_all | solution.py:32
  98.0 2.0 %reshape.825 = bf16[16,1,16,2,16,32]{5,4,3,2,1,0:T(8,128)(2,1)} reshape(bf16[16,2,8192]{2,1,0:T(2,128)(2,1)S(1)} %all-to-all-done.4) | data formatting | bytes 1048576
  100.0 2.9 %fusion.22 = bf16[8,16,32,2,16]{2,0,4,1,3:T(8,128)(2,1)S(1)} fusion(bf16[16,1,16,32,2,16]{3,5,4,2,1,0:T(8,128)(2,1)} %bitcast.191, bf16[16,1,8,2]{0,2,3,1:T(8,128)(2,1)S(1)} %get-tuple-element.14, bf16[16,1,8,2]{0,2,3,1:T(8,128)(2,1)S(1)} %get-tuple-element.13), kind=kOutput, calls=%fused_computation.38 | convolution fusion | flops 8389120 | bytes 787456 | tf_op jit(solution)/shard_map/jkcsz,jsxt->xkctz/dot_general | solution.py:132
  102.9 1.8 %fusion.25 = bf16[8,32,32,2,16]{2,1,4,0,3:T(8,128)(2,1)S(1)} fusion(bf16[8,16,32,2,16]{2,0,4,1,3:T(8,128)(2,1)S(1)} %fusion.22, bf16[16,1,32,2]{2,0,1,3:T(8,128)(2,1)S(1)} %get-tuple-element.10, bf16[16,1,32,2]{2,0,1,3:T(8,128)(2,1)S(1)} %get-tuple-element.9), kind=kOutput, calls=%fused_computation.39 | convolution fusion | flops 16785408 | bytes 790528 | tf_op jit(solution)/shard_map/xkcsz,ksyt->xyctz/dot_general | solution.py:135
  104.7 0.8 copy.49
  105.6 0.7 fusion.63
  106.3 1.1 fusion.93
  107.4 1.2 %multiply_reduce_fusion = f32[8,32,128]{2,1,0:T(8,128)S(1)} fusion(f32[8,32,32,128]{3,2,1,0:T(8,128)S(1)} %get-tuple-element.30, f32[8,32,128]{2,1,0:T(8,128)S(1)} %broadcast_multiply_fusion), kind=kLoop, calls=%fused_computation.23 | loop fusion | flops 3112960 | bytes 4456448 | tf_op jit(solution)/shard_map/reduce_sum | solution.py:99
  108.7 10.6 %fusion.21 = bf16[1,8,32,32,128]{4,3,2,1,0:T(8,128)(2,1)} fusion(f32[32]{0:T(128)S(1)} %bitcast.207, f32[32]{0:T(128)S(1)} %bitcast.208, f32[8,32,128]{2,1,0:T(8,128)S(1)} %add_rsqrt_fusion, f32[8,32,32,128]{3,2,1,0:T(8,128)S(1)} %get-tuple-element.30, f32[8,32,128]{2,1,0:T(8,128)S(1)} %broadcast_multiply_fusion), kind=kLoop, calls=%fused_computation.37 | loop fusion | flops 72351744 | bytes 6553856 | tf_op jit(solution)/shard_map/broadcast_in_dim | solution.py:146
  (26 shorter events, 0.4 us)
Async XLA Ops:
  0.0 1.6 %copy-start = (bf16[1,8,32,32,128]{4,3,2,1,0:T(8,128)(2,1)S(1)}, bf16[1,8,32,32,128]{4,3,2,1,0:T(8,128)(2,1)}, u32[]{:S(2)}) copy-start(bf16[1,8,32,32,128]{4,3,2,1,0:T(8,128)(2,1)} %param.6) | copy-start | bytes 6291460
  9.5 11.0 %all-to-all-start = ((bf16[4,2,16384]{2,1,0:T(2,128)(2,1)}), bf16[4,2,16384]{2,1,0:T(2,128)(2,1)S(1)}, u32[]{:S(2)}, u32[]{:S(2)}) async-start(bf16[4,2,16384]{2,1,0:T(2,128)(2,1)} %reshape.818), calls=%async_computation | async-start | bytes 524288 | tf_op jit(solution)/shard_map/all_to_all | solution.py:26
  22.9 19.4 %all-to-all-start.1 = ((bf16[16,2,2048]{2,1,0:T(2,128)(2,1)}), bf16[16,2,2048]{2,1,0:T(2,128)(2,1)S(1)}, u32[]{:S(2)}, u32[]{:S(2)}) async-start(bf16[16,2,2048]{2,1,0:T(2,128)(2,1)} %reshape.820), calls=%async_computation.1 | async-start | bytes 262144 | tf_op jit(solution)/shard_map/all_to_all | solution.py:26
  42.2 16.4 %all-to-all-start.2 = ((bf16[8,2,8192]{2,1,0:T(2,128)(2,1)}), bf16[8,2,8192]{2,1,0:T(2,128)(2,1)S(1)}, u32[]{:S(2)}, u32[]{:S(2)}) async-start(bf16[8,2,8192]{2,1,0:T(2,128)(2,1)} %reshape.816), calls=%async_computation.2 | async-start | bytes 524288 | tf_op jit(solution)/shard_map/all_to_all | solution.py:32
  78.8 19.2 %all-to-all-start.4 = ((bf16[16,2,8192]{2,1,0:T(2,128)(2,1)}), bf16[16,2,8192]{2,1,0:T(2,128)(2,1)S(1)}, u32[]{:S(2)}, u32[]{:S(2)}) async-start(bf16[16,2,8192]{2,1,0:T(2,128)(2,1)} %reshape.824), calls=%async_computation.4 | async-start | bytes 1048576 | tf_op jit(solution)/shard_map/all_to_all | solution.py:32
  105.5 0.8 copy-start.1
  105.5 0.8 copy-start.2
  107.4 1.3 %copy-start.3 = (f32[1,32]{1,0:T(1,128)S(1)}, f32[1,32]{1,0:T(1,128)}, u32[]{:S(2)}) copy-start(f32[1,32]{1,0:T(1,128)} %param.11) | copy-start | bytes 388
  107.4 1.3 %copy-start.4 = (f32[1,32]{1,0:T(1,128)S(1)}, f32[1,32]{1,0:T(1,128)}, u32[]{:S(2)}) copy-start(f32[1,32]{1,0:T(1,128)} %param.10) | copy-start | bytes 388
where the time goes:
time: 120 us; the launch traced here: 119 us
  waiting for transfers between devices  34.7 us (29%)
  starting transfers between devices  27.6 us (23%)
  local copies, waits for them, and re-layouts  23.2 us (19%)
  other arithmetic  12.9 us (11%)
  matrix products  12.8 us (11%)
  blocking collectives  7.8 us (6%)
    all_to_all x2, waiting for transfers between devices, copy_for_each(): return lax.all_to_all(copies, axis, split_axis=0, concat_axis=0, tiled=True)  23.4 us
    unnamed x23, local copies, waits for them, and re-layouts  17 us
    all_to_all x2, starting transfers between devices, summed_on_arrival(): lax.all_to_all(cut_along(shard, dim, length), axis, 0, 0, tiled=True)  16.1 us
    all_to_all x2, starting transfers between devices, copy_for_each(): return lax.all_to_all(copies, axis, split_axis=0, concat_axis=0, tiled=True)  11.5 us
    all_to_all x2, waiting for transfers between devices, summed_on_arrival(): lax.all_to_all(cut_along(shard, dim, length), axis, 0, 0, tiled=True)  11.3 us
    broadcast_in_dim x1, other arithmetic, local(): return hidden[None]  10.6 us
    all_to_all x1, blocking collectives, copy_for_each(): return lax.all_to_all(copies, axis, split_axis=0, concat_axis=0, tiled=True)  7.8 us
    dot_general x4, matrix products, contract(): jnp.einsum('abcz,abcdz->abdz', left, right, preferred_element_type=jnp.fl...  3.09 us
  transfers between devices with their start and end apart: 4, of which 4 were waited for; matrix products, arithmetic and copies ran while one was open for 3% of the time, Pallas kernels for 0%

commit v1 on v0

v1 whole, which is shorter than its diff:
```python
import functools
import math

import jax
import jax.numpy as jnp
import numpy as np
from jax import lax
from jax.experimental import pallas as pl
from jax.experimental.pallas import tpu as pltpu
from jax.sharding import PartitionSpec as P

MESH = pl.DeviceIdType.MESH
F32, BF16 = jnp.float32, jnp.bfloat16

N = 128
M = 16
C = 32
GX, GY, COL = 16, 4, 8
TX, TY = N // GX, N // GY
KY = M // GY
LANES = 2 * KY * M
PEER = GY * LANES
HALF = C // 2
NORM_EPS = 1e-05

FAR_X = [(dy, dz) for dz in (4, 3, 5, 2, 6, 1, 7, 0) for dy in (1, 0) if (dy, dz) != (0, 0)]
FAR_Y = (2, 1, 3)
FAR_COL = (2, 1, 3)


def signed(k):
    return np.where(k < M // 2, k, k - M)


def base_tables():
    turn = np.outer(np.arange(N), np.arange(M)) % N * (2.0 * math.pi / N)
    cosine, sine = np.tile(np.cos(turn), (1, KY)), np.tile(np.sin(turn), (1, KY))
    first = np.concatenate([cosine, -sine], axis=1)
    second = np.concatenate([-sine, -cosine], axis=1)
    return np.stack([first, second]).astype(np.float32)


def turn_tables():
    out = np.zeros((GY, 2, TY, GY, LANES), np.float32)
    for g in range(GY):
        for step in range(GY):
            ky = (g + step) % GY * KY + np.arange(KY)
            turn = np.outer(g * TY + np.arange(TY), signed(ky)) % N * (2.0 * math.pi / N)
            out[g, 0, :, step] = np.tile(np.repeat(np.cos(turn), M, axis=1), (1, 2))
            out[g, 1, :, step] = np.tile(np.repeat(np.sin(turn), M, axis=1), (1, 2))
    return out.reshape(GY, 2 * TY * GY, LANES)


def first_tables():
    f = np.arange(M // 2 + 1)
    out = np.zeros((GX, 2, f.size, TX), np.float32)
    for g in range(GX):
        turn = np.outer(f, g * TX + np.arange(TX)) % N * (2.0 * math.pi / N)
        out[g, 0], out[g, 1] = np.cos(turn), np.sin(turn)
    out = out.reshape(GX, -1, 1)
    return np.ascontiguousarray(np.broadcast_to(out, (GX, out.shape[1], LANES)))


def turned(v):
    lane = lax.broadcasted_iota(jnp.int32, v.shape, v.ndim - 1)
    swapped = pltpu.roll(v, LANES // 2, v.ndim - 1)
    return jnp.where(lane < LANES // 2, swapped, -swapped)


def modes_kernel(
    h_hbm, w_hbm, skw_hbm, par_hbm, base_hbm, turn_hbm, first_hbm,
    rows_ref, table_ref, skip_ref, affine_ref,
    hbuf, wraw, skw, par, base, turn, first,
    zsend, arecv, pm, brecv, spec, mixf, wbuf, mrecv,
    hsem, lsem, asend, arcv, bsend, brcv, csend, crcv, dsend, drcv, wsend, wrcv, vsend, vrcv,
):
    gx, gy, col = lax.axis_index("gx"), lax.axis_index("gy"), lax.axis_index("col")
    y_lo, z = gx // 8, gx % 8
    y_hi, core = col // 2, col % 2
    sibling = col + 1 - 2 * core

    def x_peer(dy, dz):
        return (y_lo + dy) % 2 * 8 + (z + dz) % 8

    def x_from(dy, dz):
        return (y_lo + dy) % 2 * 8 + (z + 8 - dz) % 8

    loads = [
        pltpu.make_async_copy(base_hbm, base, lsem.at[0]),
        pltpu.make_async_copy(turn_hbm.at[gy], turn, lsem.at[1]),
        pltpu.make_async_copy(w_hbm, wraw, lsem.at[2]),
        pltpu.make_async_copy(skw_hbm, skw, lsem.at[3]),
        pltpu.make_async_copy(par_hbm, par, lsem.at[4]),
        pltpu.make_async_copy(first_hbm.at[gx], first, lsem.at[5]),
    ]
    for cp in loads[:2]:
        cp.start()
    hload = [
        pltpu.make_async_copy(
            h_hbm.at[:, pl.ds(8 * q, 8)], hbuf.at[:, pl.ds(8 * q, 8)], hsem.at[q]
        )
        for q in range(4)
    ]
    for cp in hload:
        cp.start()
    for cp in loads[2:]:
        cp.start()

    barrier = pltpu.get_barrier_semaphore()
    for dy, dz in FAR_X:
        pl.semaphore_signal(barrier, 1, device_id={"gx": x_peer(dy, dz)}, device_id_type=MESH)
    for k in FAR_Y:
        pl.semaphore_signal(barrier, 1, device_id={"gy": (gy + k) % GY}, device_id_type=MESH)
    for k in FAR_COL:
        pl.semaphore_signal(
            barrier, 1, device_id={"col": (y_hi + k) % 4 * 2 + core}, device_id_type=MESH
        )
    pl.semaphore_signal(barrier, 1, device_id={"col": sibling}, device_id_type=MESH)

    for cp in loads[:2]:
        cp.wait()

    def table_row(y, carry):
        for k in range(GY):
            cosine = turn[pl.ds(y * GY + k, 1), :]
            sine = turn[pl.ds(TY * GY + y * GY + k, 1), :]
            table_ref[pl.ds(pl.multiple_of(y * N, N), N), k * LANES : (k + 1) * LANES] = (
                base[0] * cosine + base[1] * sine
            ).astype(BF16)
        return carry

    lax.fori_loop(0, TY, table_row, 0)
    for cp in hload:
        cp.wait()
    cells = jnp.concatenate([hbuf[:, y].reshape(TX * C, N) for y in range(TY)], axis=1)
    local = jnp.dot(cells, table_ref[...], preferred_element_type=F32)
    for k in range(GY):
        part = local[:, k * LANES : (k + 1) * LANES].astype(BF16).reshape(TX, 2, HALF, LANES)
        for half in range(2):
            zsend[k, half] = part[:, half]

    pl.semaphore_wait(barrier, len(FAR_X) + len(FAR_Y) + len(FAR_COL) + 1)

    a_copies = {}
    for half in range(2):
        for k in FAR_Y:
            a_copies[k, half] = pltpu.make_async_remote_copy(
                zsend.at[k, half], arecv.at[k - 1, half],
                asend.at[k - 1, half], arcv.at[k - 1, half],
                device_id={"gy": (gy + k) % GY}, device_id_type=MESH,
            )
            a_copies[k, half].start()

    loads[2].wait()
    for d in range(C // COL):
        block = jnp.concatenate(
            [wraw[k, s, d].astype(F32) for s in range(2) for k in range(KY)], axis=0
        )
        wbuf[col, d] = block.T.astype(BF16)
    w_copies = [
        pltpu.make_async_remote_copy(
            wbuf.at[col], wbuf.at[col], wsend.at[i], wrcv.at[i],
            device_id={"col": (y_hi + k) % 4 * 2 + core}, device_id_type=MESH,
        )
        for i, k in enumerate(FAR_COL)
    ]
    for cp in w_copies:
        cp.start()
    v_copies = [
        pltpu.make_async_remote_copy(
            wbuf.at[col], wbuf.at[col], vsend.at[3], vrcv.at[3],
            device_id={"col": sibling}, device_id_type=MESH,
        )
    ]
    v_copies[0].start()

    for cp in loads[3:]:
        cp.wait()
    wide = [jnp.broadcast_to(par[i : i + 1, :], (N, C)).T for i in range(3)]
    affine_ref[0] = wide[1]
    affine_ref[1] = wide[2]
    bias = wide[0] - jnp.mean(wide[0], axis=0, keepdims=True)
    pick = (
        lax.broadcasted_iota(jnp.int32, (C, TX * C), 1) % C
        == lax.broadcasted_iota(jnp.int32, (C, TX * C), 0)
    )
    spread = jnp.dot(skw[...], pick.astype(F32).astype(BF16), preferred_element_type=F32)
    spread = jnp.broadcast_to(spread[None], (TX, C, TX * C)).reshape(TX * C, TX * C)
    same = (
        lax.broadcasted_iota(jnp.int32, (TX * C, TX * C), 0) // C
        == lax.broadcasted_iota(jnp.int32, (TX * C, TX * C), 1) // C
    )
    diagonal = jnp.where(same, spread, 0.0).astype(BF16)

    def skip_pair(i, carry):
        pair = [hbuf[:, 2 * i + j].reshape(TX * C, N) for j in range(2)]
        out = jnp.dot(diagonal, jnp.concatenate(pair, axis=1), preferred_element_type=F32)
        for j in range(2):
            value = out[:, j * N : (j + 1) * N].reshape(TX, C, N)
            value = value - jnp.mean(value, axis=1, keepdims=True) + bias[None]
            skip_ref[2 * i + j] = value
        return carry

    lax.fori_loop(0, TY // 2, skip_pair, 0)

    b_copies = {}
    for half in range(2):
        for k in FAR_Y:
            a_copies[k, half].wait_recv()
        here, there = [], []
        for x in range(TX):
            v = zsend[0, half, x].astype(F32)
            for k in range(3):
                v = v + arecv[k, half, x].astype(F32)
            here.append(v)
            there.append(turned(v))
        for f in range(M // 2 + 1):
            even = odd = None
            for x in range(TX):
                if f == 0:
                    even = here[x] if even is None else even + here[x]
                    continue
                r = f * TX + x
                a = here[x] * first[r : r + 1, :]
                b = there[x] * first[9 * TX + r : 9 * TX + r + 1, :]
                even = a if even is None else even + a
                odd = b if odd is None else odd + b
            if f == 0:
                pm[half, 0] = even.astype(BF16)
                continue
            if f < M // 2:
                pm[half, f] = (even + odd).astype(BF16)
            pm[half, M - f] = (even - odd).astype(BF16)
        for i, (dy, dz) in enumerate(FAR_X):
            to = x_peer(dy, dz)
            b_copies[i, half] = pltpu.make_async_remote_copy(
                pm.at[half, to], brecv.at[i, half], bsend.at[i, half], brcv.at[i, half],
                device_id={"gx": to}, device_id_type=MESH,
            )
            b_copies[i, half].start()

    for i, k in enumerate(FAR_COL):
        w_copies[i].wait_recv()
        slot = (y_hi + 4 - k) % 4 * 2 + core
        v_copies.append(
            pltpu.make_async_remote_copy(
                wbuf.at[slot], wbuf.at[slot], vsend.at[i], vrcv.at[i],
                device_id={"col": sibling}, device_id_type=MESH,
            )
        )
        v_copies[-1].start()

    scale = 1.0 / math.sqrt(N * N * N)
    for half in range(2):
        total = pm[half, gx].astype(F32)
        for i in range(len(FAR_X)):
            b_copies[i, half].wait_recv()
        for i in range(len(FAR_X)):
            total = total + brecv[i, half].astype(F32)
        spec[half * HALF : (half + 1) * HALF, :] = (total * scale).astype(BF16).astype(F32)
    for cp in v_copies:
        cp.wait_recv()

    straight = spec[...]
    crossed = pltpu.roll(straight, LANES // 2, 1)
    lane = lax.broadcasted_iota(jnp.int32, (8, LANES), 1)
    for g in range(4):
        weight = wbuf[2 * g : 2 * g + 2].astype(F32).reshape(8, C, LANES)
        a = jnp.sum(weight * straight[None], axis=1)
        b = jnp.sum(weight * crossed[None], axis=1)
        mixed = jnp.where(
            lane < LANES // 2, a - pltpu.roll(a, LANES // 2, 1), b + pltpu.roll(b, LANES // 2, 1)
        )
        mixf[8 * g : 8 * g + 8, :] = mixed
    mixed = mixf[...]
    mixed = (mixed - jnp.mean(mixed, axis=0, keepdims=True)) * (1.0 / math.sqrt(M * M * M))
    mixed = mixed.astype(BF16)

    c_copies = {}
    for half in range(2):
        mrecv[gx, half] = mixed[half * HALF : (half + 1) * HALF]
        for i, (dy, dz) in enumerate(FAR_X):
            c_copies[i, half] = pltpu.make_async_remote_copy(
                mrecv.at[gx, half], mrecv.at[gx, half], csend.at[i, half], crcv.at[i, half],
                device_id={"gx": x_peer(dy, dz)}, device_id_type=MESH,
            )
            c_copies[i, half].start()

    d_copies = {}
    for half in range(2):
        for i in range(len(FAR_X)):
            c_copies[i, half].wait_recv()
        zero = mrecv[0, half].astype(F32)
        out = [zero for _ in range(TX)]
        for f in range(1, M // 2 + 1):
            low = mrecv[M - f, half].astype(F32)
            if f < M // 2:
                high = mrecv[f, half].astype(F32)
                even, odd = high + low, turned(low - high)
            else:
                even, odd = low, turned(low)
            for x in range(TX):
                r = f * TX + x
                out[x] = out[x] + even * first[r : r + 1, :]
                out[x] = out[x] + odd * first[9 * TX + r : 9 * TX + r + 1, :]
        part = pl.ds(half * HALF, HALF)
        for x in range(TX):
            rows_ref[0, x, part, :] = out[x].astype(BF16)
        for k in FAR_Y:
            d_copies[k, half] = pltpu.make_async_remote_copy(
                rows_ref.at[0, :, part, :], rows_ref.at[k, :, part, :],
                dsend.at[k - 1, half], drcv.at[k - 1, half],
                device_id={"gy": (gy + GY - k) % GY}, device_id_type=MESH,
            )
            d_copies[k, half].start()

    for cp in d_copies.values():
        cp.wait_recv()
    for cp in [*a_copies.values(), *w_copies, *b_copies.values(), *v_copies,
               *c_copies.values(), *d_copies.values()]:
        cp.wait_send()


def finish_kernel(rows_ref, table_ref, skip_ref, affine_ref, out_hbm, obuf, osem):
    rows = jnp.concatenate([rows_ref[k].reshape(TX * C, LANES) for k in range(GY)], axis=1)
    gain, shift = affine_ref[0], affine_ref[1]

    def group(i, carry):
        for p in range(2):
            y = 4 * i + 2 * p
            table = table_ref[pl.ds(pl.multiple_of(y * N, 2 * N), 2 * N), :]
            both = lax.dot_general(
                rows, table, (((1,), (1,)), ((), ())), preferred_element_type=F32
            )
            for j in range(2):
                value = both[:, j * N : (j + 1) * N].reshape(TX, C, N) + skip_ref[y + j]
                spread = jnp.mean(value * value, axis=1, keepdims=True)
                value = value * lax.rsqrt(spread + NORM_EPS) * gain[None] + shift[None]
                value = value * (lax.erf(value * math.sqrt(0.5)) + 1.0) * 0.5
                obuf[:, y + j] = value.astype(BF16)
        pltpu.make_async_copy(
            obuf.at[:, pl.ds(4 * i, 4)], out_hbm.at[:, pl.ds(4 * i, 4)], osem.at[i]
        ).start()
        return carry

    lax.fori_loop(0, TY // 4, group, 0)
    for i in range(TY // 4):
        pltpu.make_async_copy(
            obuf.at[:, pl.ds(4 * i, 4)], out_hbm.at[:, pl.ds(4 * i, 4)], osem.at[i]
        ).wait()


def local(fields, spectral, skip_weight, skip_bias, norm_gain, norm_shift):
    weights = jnp.transpose(spectral[0, 0], (0, 1, 3, 4, 2))
    params = jnp.concatenate([skip_bias, norm_gain, norm_shift], axis=0)
    dma = pltpu.SemaphoreType.DMA
    anywhere = pl.BlockSpec(memory_space=pltpu.HBM)
    vmem = pl.BlockSpec(memory_space=pltpu.VMEM)
    far_x = len(FAR_X)
    rows, table, skip, affine = pl.pallas_call(
        modes_kernel,
        name="modes",
        out_shape=[
            pltpu.VMEM((GY, TX, C, LANES), BF16),
            pltpu.VMEM((TY * N, PEER), BF16),
            pltpu.VMEM((TY, TX, C, N), F32),
            pltpu.VMEM((2, C, N), F32),
        ],
        in_specs=[anywhere] * 7,
        out_specs=[vmem] * 4,
        scratch_shapes=[
            pltpu.VMEM((TX, TY, C, N), BF16),
            pltpu.VMEM((KY, 2, C // COL, M, C), BF16),
            pltpu.VMEM((C, C), BF16),
            pltpu.VMEM((3, C), F32),
            pltpu.VMEM((2, N, LANES), F32),
            pltpu.VMEM((2 * TY * GY, LANES), F32),
            pltpu.VMEM((2 * 9 * TX, LANES), F32),
            pltpu.VMEM((GY, 2, TX, HALF, LANES), BF16),
            pltpu.VMEM((3, 2, TX, HALF, LANES), BF16),
            pltpu.VMEM((2, M, HALF, LANES), BF16),
            pltpu.VMEM((far_x, 2, HALF, LANES), BF16),
            pltpu.VMEM((C, LANES), F32),
            pltpu.VMEM((C, LANES), F32),
            pltpu.VMEM((COL, C // COL, C, LANES), BF16),
            pltpu.VMEM((GX, 2, HALF, LANES), BF16),
            dma((4,)), dma((6,)),
            dma((3, 2)), dma((3, 2)),
            dma((far_x, 2)), dma((far_x, 2)),
            dma((far_x, 2)), dma((far_x, 2)),
            dma((3, 2)), dma((3, 2)),
            dma((3,)), dma((3,)),
            dma((4,)), dma((4,)),
        ],
        compiler_params=pltpu.CompilerParams(
            collective_id=0, has_side_effects=True, vmem_limit_bytes=48 << 20
        ),
    )(
        fields[0], weights, skip_weight[0], params,
        jnp.asarray(base_tables()), jnp.asarray(turn_tables()), jnp.asarray(first_tables()),
    )
    out = pl.pallas_call(
        finish_kernel,
        name="finish",
        out_shape=jax.ShapeDtypeStruct((TX, TY, C, N), BF16),
        in_specs=[vmem] * 4,
        out_specs=anywhere,
        scratch_shapes=[pltpu.VMEM((TX, TY, C, N), BF16), dma((TY // 4,))],
        compiler_params=pltpu.CompilerParams(vmem_limit_bytes=48 << 20),
    )(rows, table, skip, affine)
    return out[None]


def solution(mesh):
    placed = (
        P("col", "gx", "gy", None, None),
        P(None, "gx", "gy", None, None, "col", None),
        P(),
        P(),
        P(),
        P(),
    )
    return jax.shard_map(
        local,
        mesh=mesh,
        in_specs=placed,
        out_specs=P("col", "gx", "gy", None, None),
        check_vma=False,
    )
```

time: 120 us -> 45.4 us (0.38)
  the two profiles are of different devices: /device:TPU:24 before, /device:TPU:2 now
where the time goes in v1:
time: 45.4 us; the launch traced here: 45.2 us
  Pallas kernels  42 us (93%)
  local copies, waits for them, and re-layouts  1.93 us (4%)
  other arithmetic  1.27 us (3%)
    pallas_call x1, Pallas kernels, local(): pl.pallas_call(modes_kernel, name='modes', out_shape=[pltpu.VMEM((GY, TX,...  34.9 us
    pallas_call x1, Pallas kernels, local(): pl.pallas_call(finish_kernel, name='finish', out_shape=jax.ShapeDtypeStru...  7.16 us
    unnamed x2, local copies, waits for them, and re-layouts  1.93 us
    concatenate x1, other arithmetic, local(): params = jnp.concatenate([skip_bias, norm_gain, norm_shift], axis=0)  1.27 us

profile of v1, /device:TPU:2, one launch (start us, length us, event | category | flops | bytes accessed | tf_op | source)
XLA Modules:
  0.0 45.2 jit_solution(16251015507993366721)
XLA Ops:
  0.0 1.3 %pad_maximum_fusion.par_hbm = f32[3,32]{1,0:T(4,128)} fusion(f32[1,32]{1,0:T(1,128)} %param.14, f32[1,32]{1,0:T(1,128)} %param.13, f32[1,32]{1,0:T(1,128)} %param.12), kind=kLoop, calls=%fused_computation | loop fusion | flops 192 | bytes 768 | tf_op jit(solution)/shard_map/concatenate | solution.py:355
  1.3 34.9 %modes.1 = (bf16[4,8,32,128]{3,2,1,0:T(8,128)(2,1)S(1)}, bf16[4096,512]{1,0:T(8,128)(2,1)S(1)}, f32[32,8,32,128]{3,2,1,0:T(8,128)S(1)}, f32[2,32,128]{2,1,0:T(8,128)S(1)}) custom-call(bf16[8,32,32,128]{3,2,1,0:T(8,128)(2,1)} %bitcast.6, bf16[4,2,4,16,32]{4,3,2,1,0:T(8,128)(2,1)} %bitcast.7, bf16[32,32]{1,0:T(8,128)(2,1)} %bitcast.8, ...), custom_call_target="tpu_custom_call" | custom-call | tf_op jit(solution)/shard_map/modes/pallas_call | solution.py:360
  36.1 0.0 copy-start
  36.2 1.9 %copy-done = f32[32,8,32,128]{3,2,1,0:T(8,128)} copy-done((f32[32,8,32,128]{3,2,1,0:T(8,128)}, f32[32,8,32,128]{3,2,1,0:T(8,128)S(1)}, u32[]{:S(2)}) %copy-start) | copy-done | bytes 4194328
  38.1 7.2 %finish.1 = bf16[8,32,32,128]{3,2,1,0:T(8,128)(2,1)} custom-call(bf16[4,8,32,128]{3,2,1,0:T(8,128)(2,1)S(1)} %get-tuple-element.9.rows_ref, bf16[4096,512]{1,0:T(8,128)(2,1)S(1)} %get-tuple-element.10.table_ref, f32[32,8,32,128]{3,2,1,0:T(8,128)} %copy-done, f32[2,32,128]{2,1,0:T(8,128)S(1)} %get-tuple-element.12.affine_ref), custom_call_target="tpu_custom_call" | custom-call | tf_op jit(solution)/shard_map/finish/pallas_call | solution.py:402
Async XLA Ops:
  36.1 1.9 %copy-start = (f32[32,8,32,128]{3,2,1,0:T(8,128)}, f32[32,8,32,128]{3,2,1,0:T(8,128)S(1)}, u32[]{:S(2)}) copy-start(f32[32,8,32,128]{3,2,1,0:T(8,128)S(1)} %get-tuple-element.11.skip_ref) | copy-start | bytes 12582916

commit v2 on v1

v2 whole, which is shorter than its diff:
```python
import functools
import math

import jax
import jax.numpy as jnp
import numpy as np
from jax import lax
from jax.experimental import pallas as pl
from jax.experimental.pallas import tpu as pltpu
from jax.sharding import PartitionSpec as P

MESH = pl.DeviceIdType.MESH
F32, BF16 = jnp.float32, jnp.bfloat16

N = 128
M = 16
C = 32
GX, GY, COL = 16, 4, 8
TX, TY = N // GX, N // GY
KY = M // GY
LANES = 2 * KY * M
PEER = GY * LANES
HALF = C // 2
NORM_EPS = 1e-05

FAR_X = [(dy, dz) for dz in (4, 3, 5, 2, 6, 1, 7, 0) for dy in (1, 0) if (dy, dz) != (0, 0)]
FAR_Y = (2, 1, 3)
FAR_COL = (2, 1, 3)
SKIP_EARLY = 4


def signed(k):
    return np.where(k < M // 2, k, k - M)


def base_tables():
    turn = np.outer(np.arange(N), np.arange(M)) % N * (2.0 * math.pi / N)
    cosine, sine = np.tile(np.cos(turn), (1, KY)), np.tile(np.sin(turn), (1, KY))
    first = np.concatenate([cosine, -sine], axis=1)
    second = np.concatenate([-sine, -cosine], axis=1)
    return np.stack([first, second]).astype(np.float32)


def turn_tables():
    out = np.zeros((GY, 2, TY, GY, LANES), np.float32)
    for g in range(GY):
        for step in range(GY):
            ky = (g + step) % GY * KY + np.arange(KY)
            turn = np.outer(g * TY + np.arange(TY), signed(ky)) % N * (2.0 * math.pi / N)
            out[g, 0, :, step] = np.tile(np.repeat(np.cos(turn), M, axis=1), (1, 2))
            out[g, 1, :, step] = np.tile(np.repeat(np.sin(turn), M, axis=1), (1, 2))
    return out.reshape(GY, 2 * TY * GY, LANES)


def first_tables():
    f = np.arange(M // 2 + 1)
    out = np.zeros((GX, 2, f.size, TX), np.float32)
    for g in range(GX):
        turn = np.outer(f, g * TX + np.arange(TX)) % N * (2.0 * math.pi / N)
        out[g, 0], out[g, 1] = np.cos(turn), np.sin(turn)
    out = out.reshape(GX, -1, 1)
    return np.ascontiguousarray(np.broadcast_to(out, (GX, out.shape[1], LANES)))


def turned(v):
    lane = lax.broadcasted_iota(jnp.int32, v.shape, v.ndim - 1)
    swapped = pltpu.roll(v, LANES // 2, v.ndim - 1)
    return jnp.where(lane < LANES // 2, swapped, -swapped)


def modes_kernel(
    h_hbm, w_hbm, skw_hbm, bias_hbm, gain_hbm, shift_hbm, base_hbm, turn_hbm, first_hbm,
    rows_ref, table_ref, skip_ref, affine_ref,
    hbuf, wraw, skw, par, base, turn, first,
    zsend, arecv, pm, brecv, spec, mixf, wbuf, mrecv,
    lsem, asend, arcv, bsend, brcv, csend, crcv, dsend, drcv, wsend, wrcv, vsend, vrcv,
):
    gx, gy, col = lax.axis_index("gx"), lax.axis_index("gy"), lax.axis_index("col")
    y_lo, z = gx // 8, gx % 8
    y_hi, core = col // 2, col % 2
    sibling = col + 1 - 2 * core

    def x_peer(dy, dz):
        return (y_lo + dy) % 2 * 8 + (z + dz) % 8

    tables = [
        pltpu.make_async_copy(base_hbm, base, lsem.at[0]),
        pltpu.make_async_copy(turn_hbm.at[gy], turn, lsem.at[1]),
    ]
    cells_in = pltpu.make_async_copy(h_hbm, hbuf, lsem.at[2])
    weights_in = pltpu.make_async_copy(w_hbm, wraw, lsem.at[3])
    loads = [
        pltpu.make_async_copy(skw_hbm, skw, lsem.at[4]),
        pltpu.make_async_copy(bias_hbm, par.at[0], lsem.at[5]),
        pltpu.make_async_copy(gain_hbm, par.at[1], lsem.at[6]),
        pltpu.make_async_copy(shift_hbm, par.at[2], lsem.at[7]),
        pltpu.make_async_copy(first_hbm.at[gx], first, lsem.at[8]),
    ]
    for cp in [*tables, cells_in, weights_in, *loads]:
        cp.start()

    def landed(ref, sem):
        pltpu.make_async_copy(ref, ref, sem).wait()

    barrier = pltpu.get_barrier_semaphore()
    for dy, dz in FAR_X:
        pl.semaphore_signal(barrier, 1, device_id={"gx": x_peer(dy, dz)}, device_id_type=MESH)
    for k in FAR_Y:
        pl.semaphore_signal(barrier, 1, device_id={"gy": (gy + k) % GY}, device_id_type=MESH)
    for k in FAR_COL:
        pl.semaphore_signal(
            barrier, 1, device_id={"col": (y_hi + k) % 4 * 2 + core}, device_id_type=MESH
        )
    pl.semaphore_signal(barrier, 1, device_id={"col": sibling}, device_id_type=MESH)

    for cp in tables:
        cp.wait()

    def table_row(y, carry):
        for k in range(GY):
            cosine = turn[pl.ds(y * GY + k, 1), :]
            sine = turn[pl.ds(TY * GY + y * GY + k, 1), :]
            table_ref[pl.ds(pl.multiple_of(y * N, N), N), k * LANES : (k + 1) * LANES] = (
                base[0] * cosine + base[1] * sine
            ).astype(BF16)
        return carry

    lax.fori_loop(0, TY, table_row, 0)
    cells_in.wait()
    cells = jnp.concatenate([hbuf[:, y].reshape(TX * C, N) for y in range(TY)], axis=1)
    local = jnp.dot(cells, table_ref[...], preferred_element_type=F32)
    for k in range(GY):
        part = local[:, k * LANES : (k + 1) * LANES].astype(BF16).reshape(TX, 2, HALF, LANES)
        for half in range(2):
            zsend[k, half] = part[:, half]

    pl.semaphore_wait(barrier, len(FAR_X) + len(FAR_Y) + len(FAR_COL) + 1)

    for half in range(2):
        for k in FAR_Y:
            pltpu.make_async_remote_copy(
                zsend.at[k, half], arecv.at[half, k - 1], asend.at[0], arcv.at[half],
                device_id={"gy": (gy + k) % GY}, device_id_type=MESH,
            ).start()

    weights_in.wait()
    for d in range(C // COL):
        block = jnp.concatenate(
            [wraw[k, s, d].astype(F32) for s in range(2) for k in range(KY)], axis=0
        )
        wbuf[col, d] = block.T.astype(BF16)
    for k in FAR_COL:
        pltpu.make_async_remote_copy(
            wbuf.at[col], wbuf.at[col], wsend.at[0], wrcv.at[0],
            device_id={"col": (y_hi + k) % 4 * 2 + core}, device_id_type=MESH,
        ).start()

    def to_sibling(slot):
        pltpu.make_async_remote_copy(
            wbuf.at[slot], wbuf.at[slot], vsend.at[0], vrcv.at[0],
            device_id={"col": sibling}, device_id_type=MESH,
        ).start()

    to_sibling(col)

    for cp in loads:
        cp.wait()
    wide = [jnp.broadcast_to(par[i], (N, C)).T for i in range(3)]
    affine_ref[0] = wide[1] * math.sqrt(0.5 * C)
    affine_ref[1] = wide[2] * math.sqrt(0.5)
    bias = wide[0] - jnp.mean(wide[0], axis=0, keepdims=True)
    pick = (
        lax.broadcasted_iota(jnp.int32, (C, TX * C), 1) % C
        == lax.broadcasted_iota(jnp.int32, (C, TX * C), 0)
    )
    spread = jnp.dot(skw[...], pick.astype(F32).astype(BF16), preferred_element_type=F32)
    spread = jnp.broadcast_to(spread[None], (TX, C, TX * C)).reshape(TX * C, TX * C)
    same = (
        lax.broadcasted_iota(jnp.int32, (TX * C, TX * C), 0) // C
        == lax.broadcasted_iota(jnp.int32, (TX * C, TX * C), 1) // C
    )
    diagonal = jnp.where(same, spread, 0.0).astype(BF16)

    def skip_rows(i, carry):
        four = [hbuf[:, 4 * i + j].reshape(TX * C, N) for j in range(4)]
        out = jnp.dot(diagonal, jnp.concatenate(four, axis=1), preferred_element_type=F32)
        for j in range(4):
            value = out[:, j * N : (j + 1) * N].reshape(TX, C, N)
            value = value - jnp.mean(value, axis=1, keepdims=True) + bias[None]
            skip_ref[4 * i + j] = value
        return carry

    lax.fori_loop(0, SKIP_EARLY, skip_rows, 0)

    for half in range(2):
        landed(arecv.at[half], arcv.at[half])
        here, there = [], []
        for x in range(TX):
            v = zsend[0, half, x].astype(F32)
            for k in range(3):
                v = v + arecv[half, k, x].astype(F32)
            here.append(v)
            there.append(turned(v))
        for f in range(M // 2 + 1):
            even = odd = None
            for x in range(TX):
                if f == 0:
                    even = here[x] if even is None else even + here[x]
                    continue
                r = f * TX + x
                a = here[x] * first[r : r + 1, :]
                b = there[x] * first[9 * TX + r : 9 * TX + r + 1, :]
                even = a if even is None else even + a
                odd = b if odd is None else odd + b
            if f == 0:
                pm[half, 0] = even.astype(BF16)
                continue
            if f < M // 2:
                pm[half, f] = (even + odd).astype(BF16)
            pm[half, M - f] = (even - odd).astype(BF16)
        for i, (dy, dz) in enumerate(FAR_X):
            to = x_peer(dy, dz)
            pltpu.make_async_remote_copy(
                pm.at[half, to], brecv.at[half, i], bsend.at[0], brcv.at[half],
                device_id={"gx": to}, device_id_type=MESH,
            ).start()

    lax.fori_loop(SKIP_EARLY, TY // 4, skip_rows, 0)

    landed(wbuf.at[0:3], wrcv.at[0])
    for k in FAR_COL:
        to_sibling((y_hi + 4 - k) % 4 * 2 + core)

    scale = 1.0 / math.sqrt(N * N * N)
    for half in range(2):
        total = pm[half, gx].astype(F32)
        landed(brecv.at[half], brcv.at[half])
        for i in range(len(FAR_X)):
            total = total + brecv[half, i].astype(F32)
        spec[half * HALF : (half + 1) * HALF, :] = (total * scale).astype(BF16).astype(F32)
    landed(wbuf.at[0:4], vrcv.at[0])

    straight = spec[...]
    crossed = pltpu.roll(straight, LANES // 2, 1)
    lane = lax.broadcasted_iota(jnp.int32, (8, LANES), 1)
    for g in range(4):
        weight = wbuf[2 * g : 2 * g + 2].astype(F32).reshape(8, C, LANES)
        a = jnp.sum(weight * straight[None], axis=1)
        b = jnp.sum(weight * crossed[None], axis=1)
        mixed = jnp.where(
            lane < LANES // 2, a - pltpu.roll(a, LANES // 2, 1), b + pltpu.roll(b, LANES // 2, 1)
        )
        mixf[8 * g : 8 * g + 8, :] = mixed
    mixed = mixf[...]
    mixed = (mixed - jnp.mean(mixed, axis=0, keepdims=True)) * (1.0 / math.sqrt(M * M * M))
    mixed = mixed.astype(BF16)

    mrecv[gx] = mixed
    for dy, dz in FAR_X:
        pltpu.make_async_remote_copy(
            mrecv.at[gx], mrecv.at[gx], csend.at[0], crcv.at[0],
            device_id={"gx": x_peer(dy, dz)}, device_id_type=MESH,
        ).start()

    landed(mrecv.at[0 : GX - 1], crcv.at[0])
    for half in range(2):
        part = slice(half * HALF, (half + 1) * HALF)
        zero = mrecv[0, part].astype(F32)
        out = [zero for _ in range(TX)]
        for f in range(1, M // 2 + 1):
            low = mrecv[M - f, part].astype(F32)
            if f < M // 2:
                high = mrecv[f, part].astype(F32)
                even, odd = high + low, turned(low - high)
            else:
                even, odd = low, turned(low)
            for x in range(TX):
                r = f * TX + x
                out[x] = out[x] + even * first[r : r + 1, :]
                out[x] = out[x] + odd * first[9 * TX + r : 9 * TX + r + 1, :]
        for x in range(TX):
            rows_ref[0, x, part, :] = out[x].astype(BF16)
        for k in FAR_Y:
            span = pl.ds(half * HALF, HALF)
            pltpu.make_async_remote_copy(
                rows_ref.at[0, :, span, :], rows_ref.at[k, :, span, :], dsend.at[0], drcv.at[0],
                device_id={"gy": (gy + GY - k) % GY}, device_id_type=MESH,
            ).start()

    landed(zsend.at[1:4], asend.at[0])
    landed(wbuf.at[0:3], wsend.at[0])
    landed(wbuf.at[0:4], vsend.at[0])
    landed(brecv, bsend.at[0])
    landed(mrecv.at[0 : GX - 1], csend.at[0])
    landed(rows_ref.at[1:4], dsend.at[0])
    landed(rows_ref.at[1:4], drcv.at[0])


def finish_kernel(rows_ref, table_ref, skip_ref, affine_ref, out_hbm, obuf, acc, osem):
    rows = jnp.concatenate([rows_ref[k].reshape(TX * C, LANES) for k in range(GY)], axis=1)
    gain, shift = affine_ref[0], affine_ref[1]

    def transform(i, slot):
        for p in range(2):
            y = 4 * i + 2 * p
            table = table_ref[pl.ds(pl.multiple_of(y * N, 2 * N), 2 * N), :]
            both = lax.dot_general(
                rows, table, (((1,), (1,)), ((), ())), preferred_element_type=F32
            )
            for j in range(2):
                acc[slot, 2 * p + j] = both[:, j * N : (j + 1) * N].reshape(TX, C, N)

    def settle(i, slot):
        for j in range(4):
            value = acc[slot, j] + skip_ref[4 * i + j]
            spread = jnp.sum(value * value, axis=1, keepdims=True)
            value = value * lax.rsqrt(spread + C * NORM_EPS) * gain[None] + shift[None]
            value = (value * math.sqrt(0.5)) * (lax.erf(value) + 1.0)
            obuf[:, 4 * i + j] = value.astype(BF16)
        written(i).start()

    def written(i):
        span = pl.ds(4 * i, 4)
        return pltpu.make_async_copy(obuf.at[:, span], out_hbm.at[:, span], osem.at[0])

    transform(0, 0)

    def two(i, carry):
        transform(2 * i + 1, 1)
        settle(2 * i, 0)
        transform(jnp.minimum(2 * i + 2, TY // 4 - 1), 0)
        settle(2 * i + 1, 1)
        return carry

    lax.fori_loop(0, TY // 8, two, 0)
    pltpu.make_async_copy(obuf, out_hbm, osem.at[0]).wait()


def local(fields, spectral, skip_weight, skip_bias, norm_gain, norm_shift):
    weights = jnp.transpose(spectral[0, 0], (0, 1, 3, 4, 2))
    dma = pltpu.SemaphoreType.DMA
    anywhere = pl.BlockSpec(memory_space=pltpu.HBM)
    vmem = pl.BlockSpec(memory_space=pltpu.VMEM)
    far_x = len(FAR_X)
    rows, table, skip, affine = pl.pallas_call(
        modes_kernel,
        name="modes",
        out_shape=[
            pltpu.VMEM((GY, TX, C, LANES), BF16),
            pltpu.VMEM((TY * N, PEER), BF16),
            pltpu.VMEM((TY, TX, C, N), F32),
            pltpu.VMEM((2, C, N), F32),
        ],
        in_specs=[anywhere] * 9,
        out_specs=[vmem] * 4,
        scratch_shapes=[
            pltpu.VMEM((TX, TY, C, N), BF16),
            pltpu.VMEM((KY, 2, C // COL, M, C), BF16),
            pltpu.VMEM((C, C), BF16),
            pltpu.VMEM((3, 1, C), F32),
            pltpu.VMEM((2, N, LANES), F32),
            pltpu.VMEM((2 * TY * GY, LANES), F32),
            pltpu.VMEM((2 * 9 * TX, LANES), F32),
            pltpu.VMEM((GY, 2, TX, HALF, LANES), BF16),
            pltpu.VMEM((2, 3, TX, HALF, LANES), BF16),
            pltpu.VMEM((2, M, HALF, LANES), BF16),
            pltpu.VMEM((2, far_x, HALF, LANES), BF16),
            pltpu.VMEM((C, LANES), F32),
            pltpu.VMEM((C, LANES), F32),
            pltpu.VMEM((COL, C // COL, C, LANES), BF16),
            pltpu.VMEM((GX, C, LANES), BF16),
            dma((9,)),
            dma((1,)), dma((2,)),
            dma((1,)), dma((2,)),
            dma((1,)), dma((1,)),
            dma((1,)), dma((1,)),
            dma((1,)), dma((1,)),
            dma((1,)), dma((1,)),
        ],
        compiler_params=pltpu.CompilerParams(
            collective_id=0, has_side_effects=True, vmem_limit_bytes=48 << 20
        ),
    )(
        fields[0], weights, skip_weight[0], skip_bias, norm_gain, norm_shift,
        jnp.asarray(base_tables()), jnp.asarray(turn_tables()), jnp.asarray(first_tables()),
    )
    out = pl.pallas_call(
        finish_kernel,
        name="finish",
        out_shape=jax.ShapeDtypeStruct((TX, TY, C, N), BF16),
        in_specs=[vmem] * 4,
        out_specs=anywhere,
        scratch_shapes=[
            pltpu.VMEM((TX, TY, C, N), BF16),
            pltpu.VMEM((2, 4, TX, C, N), F32),
            dma((1,)),
        ],
        compiler_params=pltpu.CompilerParams(vmem_limit_bytes=16 << 20),
    )(rows, table, skip, affine)
    return out[None]


def solution(mesh):
    placed = (
        P("col", "gx", "gy", None, None),
        P(None, "gx", "gy", None, None, "col", None),
        P(),
        P(),
        P(),
        P(),
    )
    return jax.shard_map(
        local,
        mesh=mesh,
        in_specs=placed,
        out_specs=P("col", "gx", "gy", None, None),
        check_vma=False,
    )
```

time: 45.4 us -> 37.7 us (0.83)
  Pallas kernels: 42 us -> 37.6 us
  local copies, waits for them, and re-layouts: 1.93 us -> 0 us
  other arithmetic: 1.27 us -> 0 us
    pallas_call x1, Pallas kernels: 7.16 us -> 3.98 us  [local(): pl.pallas_call(finish_kernel, name='finish', out_shape=jax.ShapeDtypeStru...]
    unnamed x2 -> x0, local copies, waits for them, and re-layouts: 1.93 us -> none
    pallas_call x1, Pallas kernels: 34.9 us -> 33.6 us  [local(): pl.pallas_call(modes_kernel, name='modes', out_shape=[pltpu.VMEM((GY, TX,...]
    concatenate x1 -> x0, other arithmetic: 1.27 us -> none  [local(): params = jnp.concatenate([skip_bias, norm_gain, norm_shift], axis=0)]
where the time goes in v2:
time: 37.7 us; the launch traced here: 37.6 us
  Pallas kernels  37.6 us (100%)
    pallas_call x1, Pallas kernels, local(): pl.pallas_call(modes_kernel, name='modes', out_shape=[pltpu.VMEM((GY, TX,...  33.6 us
    pallas_call x1, Pallas kernels, local(): pl.pallas_call(finish_kernel, name='finish', out_shape=jax.ShapeDtypeStru...  3.98 us

profile of v2, /device:TPU:2, one launch (start us, length us, event | category | flops | bytes accessed | tf_op | source)
XLA Modules:
  0.0 37.6 jit_solution(1506817365722915840)
XLA Ops:
  0.0 33.6 %modes.1 = (bf16[4,8,32,128]{3,2,1,0:T(8,128)(2,1)S(1)}, bf16[4096,512]{1,0:T(8,128)(2,1)S(1)}, f32[32,8,32,128]{3,2,1,0:T(8,128)S(1)}, f32[2,32,128]{2,1,0:T(8,128)S(1)}) custom-call(bf16[8,32,32,128]{3,2,1,0:T(8,128)(2,1)} %bitcast.6, bf16[4,2,4,16,32]{4,3,2,1,0:T(8,128)(2,1)} %bitcast.7, bf16[32,32]{1,0:T(8,128)(2,1)} %bitcast.8, f32[1,32]{1,0:T(1,128)} %bias_hbm.1, ...), custom_call_target="tpu_custom_call" | custom-call | tf_op jit(solution)/shard_map/modes/pallas_call | solution.py:345
  33.6 4.0 %finish.1 = bf16[8,32,32,128]{3,2,1,0:T(8,128)(2,1)} custom-call(bf16[4,8,32,128]{3,2,1,0:T(8,128)(2,1)S(1)} %get-tuple-element.9.rows_ref, bf16[4096,512]{1,0:T(8,128)(2,1)S(1)} %get-tuple-element.10.table_ref, f32[32,8,32,128]{3,2,1,0:T(8,128)S(1)} %get-tuple-element.11.skip_ref, f32[2,32,128]{2,1,0:T(8,128)S(1)} %get-tuple-element.12.affine_ref), custom_call_target="tpu_custom_call" | custom-call | tf_op jit(solution)/shard_map/finish/pallas_call | solution.py:387

commit v3 on v2

--- a/solution.py
+++ b/solution.py
@@ -21,12 +21,14 @@
 LANES = 2 * KY * M
 PEER = GY * LANES
 HALF = C // 2
+XH = TX // 2
 NORM_EPS = 1e-05
 
 FAR_X = [(dy, dz) for dz in (4, 3, 5, 2, 6, 1, 7, 0) for dy in (1, 0) if (dy, dz) != (0, 0)]
 FAR_Y = (2, 1, 3)
 FAR_COL = (2, 1, 3)
-SKIP_EARLY = 4
+EARLY_ROWS = 14
+WRITE = 4
 
 
 def signed(k):
@@ -70,8 +72,8 @@
 
 def modes_kernel(
     h_hbm, w_hbm, skw_hbm, bias_hbm, gain_hbm, shift_hbm, base_hbm, turn_hbm, first_hbm,
-    rows_ref, table_ref, skip_ref, affine_ref,
-    hbuf, wraw, skw, par, base, turn, first,
+    rows_late, back_ref, skip_late, affine_ref, out_early,
+    rows_early, skip_early, table, hbuf, wraw, skw, par, base, turn, first,
     zsend, arecv, pm, brecv, spec, mixf, wbuf, mrecv,
     lsem, asend, arcv, bsend, brcv, csend, crcv, dsend, drcv, wsend, wrcv, vsend, vrcv,
 ):
@@ -116,19 +118,20 @@
     for cp in tables:
         cp.wait()
 
-    def table_row(y, carry):
+    def table_row(y):
         for k in range(GY):
-            cosine = turn[pl.ds(y * GY + k, 1), :]
-            sine = turn[pl.ds(TY * GY + y * GY + k, 1), :]
-            table_ref[pl.ds(pl.multiple_of(y * N, N), N), k * LANES : (k + 1) * LANES] = (
-                base[0] * cosine + base[1] * sine
-            ).astype(BF16)
-        return carry
-
-    lax.fori_loop(0, TY, table_row, 0)
+            cosine = turn[y * GY + k : y * GY + k + 1, :]
+            sine = turn[(TY + y) * GY + k : (TY + y) * GY + k + 1, :]
+            table[y, k] = (base[0] * cosine + base[1] * sine).astype(BF16)
+
+    for y in range(EARLY_ROWS):
+        table_row(y)
     cells_in.wait()
+    for y in range(EARLY_ROWS, TY):
+        table_row(y)
     cells = jnp.concatenate([hbuf[:, y].reshape(TX * C, N) for y in range(TY)], axis=1)
-    local = jnp.dot(cells, table_ref[...], preferred_element_type=F32)
+    steps = [table[:, k].reshape(TY * N, LANES) for k in range(GY)]
+    local = jnp.dot(cells, jnp.concatenate(steps, axis=1), preferred_element_type=F32)
     for k in range(GY):
         part = local[:, k * LANES : (k + 1) * LANES].astype(BF16).reshape(TX, 2, HALF, LANES)
         for half in range(2):
@@ -187,10 +190,11 @@
         for j in range(4):
             value = out[:, j * N : (j + 1) * N].reshape(TX, C, N)
             value = value - jnp.mean(value, axis=1, keepdims=True) + bias[None]
-            skip_ref[4 * i + j] = value
+            skip_early[4 * i + j] = value[:XH]
+            skip_late[4 * i + j] = value[XH:]
         return carry
 
-    lax.fori_loop(0, SKIP_EARLY, skip_rows, 0)
+    lax.fori_loop(0, TY // 4, skip_rows, 0)
 
     for half in range(2):
         landed(arecv.at[half], arcv.at[half])
@@ -225,8 +229,6 @@
                 device_id={"gx": to}, device_id_type=MESH,
             ).start()
 
-    lax.fori_loop(SKIP_EARLY, TY // 4, skip_rows, 0)
-
     landed(wbuf.at[0:3], wrcv.at[0])
     for k in FAR_COL:
         to_sibling((y_hi + 4 - k) % 4 * 2 + core)
@@ -262,78 +264,80 @@
             device_id={"gx": x_peer(dy, dz)}, device_id_type=MESH,
         ).start()
 
+    def table_column(y, carry):
+        for k in range(GY):
+            back_ref[y, k] = table[y, k].T
+        return carry
+
+    lax.fori_loop(0, TY, table_column, 0)
+
     landed(mrecv.at[0 : GX - 1], crcv.at[0])
-    for half in range(2):
-        part = slice(half * HALF, (half + 1) * HALF)
-        zero = mrecv[0, part].astype(F32)
-        out = [zero for _ in range(TX)]
-        for f in range(1, M // 2 + 1):
-            low = mrecv[M - f, part].astype(F32)
-            if f < M // 2:
-                high = mrecv[f, part].astype(F32)
-                even, odd = high + low, turned(low - high)
-            else:
-                even, odd = low, turned(low)
-            for x in range(TX):
-                r = f * TX + x
-                out[x] = out[x] + even * first[r : r + 1, :]
-                out[x] = out[x] + odd * first[9 * TX + r : 9 * TX + r + 1, :]
-        for x in range(TX):
-            rows_ref[0, x, part, :] = out[x].astype(BF16)
+    for late, rows in enumerate((rows_early, rows_late)):
+        for half in range(2):
+            part = slice(half * HALF, (half + 1) * HALF)
+            zero = mrecv[0, part].astype(F32)
+            out = [zero for _ in range(XH)]
+            for f in range(1, M // 2 + 1):
+                low = mrecv[M - f, part].astype(F32)
+                if f < M // 2:
+                    high = mrecv[f, part].astype(F32)
+                    even, odd = high + low, turned(low - high)
+                else:
+                    even, odd = low, turned(low)
+                for x in range(XH):
+                    r = f * TX + late * XH + x
+                    out[x] = out[x] + even * first[r : r + 1, :]
+                    out[x] = out[x] + odd * first[9 * TX + r : 9 * TX + r + 1, :]
+            for x in range(XH):
+                rows[0, x, part, :] = out[x].astype(BF16)
         for k in FAR_Y:
-            span = pl.ds(half * HALF, HALF)
             pltpu.make_async_remote_copy(
-                rows_ref.at[0, :, span, :], rows_ref.at[k, :, span, :], dsend.at[0], drcv.at[0],
+                rows.at[0], rows.at[k], dsend.at[0], drcv.at[late],
                 device_id={"gy": (gy + GY - k) % GY}, device_id_type=MESH,
             ).start()
+
+    landed(rows_early.at[1:4], drcv.at[0])
+    settle(rows_early, back_ref, skip_early, affine_ref, out_early)
 
     landed(zsend.at[1:4], asend.at[0])
     landed(wbuf.at[0:3], wsend.at[0])
     landed(wbuf.at[0:4], vsend.at[0])
     landed(brecv, bsend.at[0])
     landed(mrecv.at[0 : GX - 1], csend.at[0])
-    landed(rows_ref.at[1:4], dsend.at[0])
-    landed(rows_ref.at[1:4], drcv.at[0])
-
-
-def finish_kernel(rows_ref, table_ref, skip_ref, affine_ref, out_hbm, obuf, acc, osem):
-    rows = jnp.concatenate([rows_ref[k].reshape(TX * C, LANES) for k in range(GY)], axis=1)
-    gain, shift = affine_ref[0], affine_ref[1]
-
-    def transform(i, slot):
-        for p in range(2):
-            y = 4 * i + 2 * p
-            table = table_ref[pl.ds(pl.multiple_of(y * N, 2 * N), 2 * N), :]
-            both = lax.dot_general(
-                rows, table, (((1,), (1,)), ((), ())), preferred_element_type=F32
-            )
-            for j in range(2):
-                acc[slot, 2 * p + j] = both[:, j * N : (j + 1) * N].reshape(TX, C, N)
-
-    def settle(i, slot):
-        for j in range(4):
-            value = acc[slot, j] + skip_ref[4 * i + j]
-            spread = jnp.sum(value * value, axis=1, keepdims=True)
-            value = value * lax.rsqrt(spread + C * NORM_EPS) * gain[None] + shift[None]
-            value = (value * math.sqrt(0.5)) * (lax.erf(value) + 1.0)
-            obuf[:, 4 * i + j] = value.astype(BF16)
-        written(i).start()
-
-    def written(i):
-        span = pl.ds(4 * i, 4)
-        return pltpu.make_async_copy(obuf.at[:, span], out_hbm.at[:, span], osem.at[0])
-
-    transform(0, 0)
-
-    def two(i, carry):
-        transform(2 * i + 1, 1)
-        settle(2 * i, 0)
-        transform(jnp.minimum(2 * i + 2, TY // 4 - 1), 0)
-        settle(2 * i + 1, 1)
-        return carry
-
-    lax.fori_loop(0, TY // 8, two, 0)
-    pltpu.make_async_copy(obuf, out_hbm, osem.at[0]).wait()
+    landed(zsend.at[1:4], dsend.at[0])
+    landed(rows_late.at[1:4], drcv.at[1])
+
+
+def settle(rows_ref, back_ref, skip_ref, affine_ref, out_ref, written=None):
+    rows = jnp.concatenate([rows_ref[k].reshape(XH * C, LANES) for k in range(GY)], axis=1)
+    for y in range(0, TY, 2):
+        back = [back_ref[y + j].reshape(PEER, N) for j in range(2)]
+        both = jnp.dot(rows, jnp.concatenate(back, axis=1), preferred_element_type=F32)
+        for j in range(2):
+            for x in range(XH):
+                value = both[x * C : (x + 1) * C, j * N : (j + 1) * N] + skip_ref[y + j, x]
+                spread = jnp.sum(value * value, axis=0, keepdims=True)
+                value = value * lax.rsqrt(spread + C * NORM_EPS) * affine_ref[0] + affine_ref[1]
+                value = (value * math.sqrt(0.5)) * (lax.erf(value) + 1.0)
+                out_ref[x, y + j] = value.astype(BF16)
+        if written is not None and y % WRITE == WRITE - 2:
+            written(pl.ds(y + 2 - WRITE, WRITE))
+
+
+def finish_kernel(
+    rows_late, back_ref, skip_late, affine_ref, out_early, out_hbm, out_late, early_sem, late_sem
+):
+    early = pltpu.make_async_copy(out_early, out_hbm.at[0:XH], early_sem.at[0])
+    early.start()
+
+    def written(span):
+        pltpu.make_async_copy(
+            out_late.at[:, span], out_hbm.at[XH:TX, span], late_sem.at[0]
+        ).start()
+
+    settle(rows_late, back_ref, skip_late, affine_ref, out_late, written)
+    early.wait()
+    pltpu.make_async_copy(out_late, out_hbm.at[XH:TX], late_sem.at[0]).wait()
 
 
 def local(fields, spectral, skip_weight, skip_bias, norm_gain, norm_shift):
@@ -342,18 +346,22 @@
     anywhere = pl.BlockSpec(memory_space=pltpu.HBM)
     vmem = pl.BlockSpec(memory_space=pltpu.VMEM)
     far_x = len(FAR_X)
-    rows, table, skip, affine = pl.pallas_call(
+    rows, back, skip, affine, early = pl.pallas_call(
         modes_kernel,
         name="modes",
         out_shape=[
-            pltpu.VMEM((GY, TX, C, LANES), BF16),
-            pltpu.VMEM((TY * N, PEER), BF16),
-            pltpu.VMEM((TY, TX, C, N), F32),
+            pltpu.VMEM((GY, XH, C, LANES), BF16),
+            pltpu.VMEM((TY, GY, LANES, N), BF16),
+            pltpu.VMEM((TY, XH, C, N), F32),
             pltpu.VMEM((2, C, N), F32),
+            pltpu.VMEM((XH, TY, C, N), BF16),
         ],
         in_specs=[anywhere] * 9,
-        out_specs=[vmem] * 4,
+        out_specs=[vmem] * 5,
         scratch_shapes=[
+            pltpu.VMEM((GY, XH, C, LANES), BF16),
+            pltpu.VMEM((TY, XH, C, N), F32),
+            pltpu.VMEM((TY, GY, N, LANES), BF16),
             pltpu.VMEM((TX, TY, C, N), BF16),
             pltpu.VMEM((KY, 2, C // COL, M, C), BF16),
             pltpu.VMEM((C, C), BF16),
@@ -373,7 +381,7 @@
             dma((1,)), dma((2,)),
             dma((1,)), dma((2,)),
             dma((1,)), dma((1,)),
-            dma((1,)), dma((1,)),
+            dma((1,)), dma((2,)),
             dma((1,)), dma((1,)),
             dma((1,)), dma((1,)),
         ],
@@ -388,15 +396,11 @@
         finish_kernel,
         name="finish",
         out_shape=jax.ShapeDtypeStruct((TX, TY, C, N), BF16),
-        in_specs=[vmem] * 4,
+        in_specs=[vmem] * 5,
         out_specs=anywhere,
-        scratch_shapes=[
-            pltpu.VMEM((TX, TY, C, N), BF16),
-            pltpu.VMEM((2, 4, TX, C, N), F32),
-            dma((1,)),
-        ],
+        scratch_shapes=[pltpu.VMEM((XH, TY, C, N), BF16), dma((1,)), dma((1,))],
         compiler_params=pltpu.CompilerParams(vmem_limit_bytes=16 << 20),
-    )(rows, table, skip, affine)
+    )(rows, back, skip, affine, early)
     return out[None]
 
 

time: 37.7 us -> 36.3 us (0.963)
  Pallas kernels: 37.6 us -> 36.1 us
    pallas_call x1, Pallas kernels: 3.98 us -> 1.93 us  [local(): pl.pallas_call(finish_kernel, name='finish', out_shape=jax.ShapeDtypeStru...]
    pallas_call x1, Pallas kernels: 33.6 us -> 34.2 us  [local(): pl.pallas_call(modes_kernel, name='modes', out_shape=[pltpu.VMEM((GY, XH,...]
where the time goes in v3:
time: 36.3 us; the launch traced here: 36.1 us
  Pallas kernels  36.1 us (99%)
    pallas_call x1, Pallas kernels, local(): pl.pallas_call(modes_kernel, name='modes', out_shape=[pltpu.VMEM((GY, XH,...  34.2 us
    pallas_call x1, Pallas kernels, local(): pl.pallas_call(finish_kernel, name='finish', out_shape=jax.ShapeDtypeStru...  1.93 us

profile of v3, /device:TPU:2, one launch (start us, length us, event | category | flops | bytes accessed | tf_op | source)
XLA Modules:
  0.0 36.1 jit_solution(7598454430387186650)
XLA Ops:
  0.0 34.2 %modes.1 = (bf16[4,4,32,128]{3,2,1,0:T(8,128)(2,1)S(1)}, bf16[32,4,128,128]{3,2,1,0:T(8,128)(2,1)S(1)}, f32[32,4,32,128]{3,2,1,0:T(8,128)S(1)}, f32[2,32,128]{2,1,0:T(8,128)S(1)}, bf16[4,32,32,128]{3,2,1,0:T(8,128)(2,1)S(1)}) custom-call(bf16[8,32,32,128]{3,2,1,0:T(8,128)(2,1)} %bitcast.6, bf16[4,2,4,16,32]{4,3,2,1,0:T(8,128)(2,1)} %bitcast.7, ...), custom_call_target="tpu_custom_call" | custom-call | tf_op jit(solution)/shard_map/modes/pallas_call | solution.py:349
  34.2 1.9 %finish.1 = bf16[8,32,32,128]{3,2,1,0:T(8,128)(2,1)} custom-call(bf16[4,4,32,128]{3,2,1,0:T(8,128)(2,1)S(1)} %get-tuple-element.10.rows_late, bf16[32,4,128,128]{3,2,1,0:T(8,128)(2,1)S(1)} %get-tuple-element.11.back_ref, f32[32,4,32,128]{3,2,1,0:T(8,128)S(1)} %get-tuple-element.12.skip_late, f32[2,32,128]{2,1,0:T(8,128)S(1)} %get-tuple-element.13.affine_ref, ...), custom_call_target="tpu_custom_call" | custom-call | tf_op jit(solution)/shard_map/finish/pallas_call | solution.py:395

commit v4 on v3

--- a/solution.py
+++ b/solution.py
@@ -24,7 +24,7 @@
 XH = TX // 2
 NORM_EPS = 1e-05
 
-FAR_X = [(dy, dz) for dz in (4, 3, 5, 2, 6, 1, 7, 0) for dy in (1, 0) if (dy, dz) != (0, 0)]
+FAR_X = [(dy, dz) for dy in (1, 0) for dz in (4, 3, 5, 2, 6, 1, 7, 0) if (dy, dz) != (0, 0)]
 FAR_Y = (2, 1, 3)
 FAR_COL = (2, 1, 3)
 EARLY_ROWS = 14

time: 36.3 us -> 36.3 us (level)
  no operation moved by 1% of the time
where the time goes in v4:
time: 36.3 us; the launch traced here: 36.1 us
  Pallas kernels  36.1 us (99%)
    pallas_call x1, Pallas kernels, local(): pl.pallas_call(modes_kernel, name='modes', out_shape=[pltpu.VMEM((GY, XH,...  34.2 us
    pallas_call x1, Pallas kernels, local(): pl.pallas_call(finish_kernel, name='finish', out_shape=jax.ShapeDtypeStru...  1.93 us

profile of v4, /device:TPU:2, one launch (start us, length us, event | category | flops | bytes accessed | tf_op | source)
XLA Modules:
  0.0 36.1 jit_solution(872929266299822359)
XLA Ops:
  0.0 34.2 %modes.1 = (bf16[4,4,32,128]{3,2,1,0:T(8,128)(2,1)S(1)}, bf16[32,4,128,128]{3,2,1,0:T(8,128)(2,1)S(1)}, f32[32,4,32,128]{3,2,1,0:T(8,128)S(1)}, f32[2,32,128]{2,1,0:T(8,128)S(1)}, bf16[4,32,32,128]{3,2,1,0:T(8,128)(2,1)S(1)}) custom-call(bf16[8,32,32,128]{3,2,1,0:T(8,128)(2,1)} %bitcast.6, bf16[4,2,4,16,32]{4,3,2,1,0:T(8,128)(2,1)} %bitcast.7, ...), custom_call_target="tpu_custom_call" | custom-call | tf_op jit(solution)/shard_map/modes/pallas_call | solution.py:349
  34.2 1.9 %finish.1 = bf16[8,32,32,128]{3,2,1,0:T(8,128)(2,1)} custom-call(bf16[4,4,32,128]{3,2,1,0:T(8,128)(2,1)S(1)} %get-tuple-element.10.rows_late, bf16[32,4,128,128]{3,2,1,0:T(8,128)(2,1)S(1)} %get-tuple-element.11.back_ref, f32[32,4,32,128]{3,2,1,0:T(8,128)S(1)} %get-tuple-element.12.skip_late, f32[2,32,128]{2,1,0:T(8,128)S(1)} %get-tuple-element.13.affine_ref, ...), custom_call_target="tpu_custom_call" | custom-call | tf_op jit(solution)/shard_map/finish/pallas_call | solution.py:395
